TPU v7x, 32 devices: a whole 2x2x4 slice. The times are simulated.
32 devices in a mesh: dom: 16 (over z, x, core), vec: 2 (over y).
Axes of the slice: x: 2, y: 2, z: 4, core: 2. Of those that a mesh axis runs over, the one named last changes fastest.
Arguments:
- orbitals: bfloat16 [128, 65536], P(None, ('dom', 'vec'))
- projectors: bfloat16 [65536, 512], P('dom', 'vec'), may hold values from -0.0234375 to 0.0234375
- potential: float32 [65536], P(('dom', 'vec')), may hold values from 0 to 2
Outputs:
- filtered: bfloat16 [128, 65536], P(None, ('dom', 'vec'))
All inputs are finite; a program needn't handle non-finite values.
Results may differ from a plain program's by a relative error of at most 0.0052.
Values may be sent and summed in bfloat16 or wider, within the bound.
No kernel may reach another device: no remote copies, remote signals or barrier semaphores. Data moves between devices by JAX's collectives and lax.ppermute only.
A program may use at most 64 MiB of HBM per device.

v0:
```python
import jax
import jax.numpy as jnp
from jax import lax
from jax.sharding import PartitionSpec as P

CENTER = 1.0
HALF_WIDTH = 1.5
EPSILON = 1e-06


def hamiltonian(bands_now, projectors, shifted):
    partial_sum = jnp.dot(
        lax.all_gather(bands_now, "vec", axis=1, tiled=True),
        projectors,
        preferred_element_type=jnp.float32,
    )
    intersection_b = lax.psum(partial_sum, "dom").astype(jnp.bfloat16)
    action_terms = lax.dot_general(
        intersection_b, projectors, (((1,), (1,)), ((), ())), preferred_element_type=jnp.float32
    )
    actions = lax.psum_scatter(action_terms, "vec", scatter_dimension=1, tiled=True)
    return (shifted[None, :] * bands_now.astype(jnp.float32) - actions) / HALF_WIDTH


def chebyshev(bands_now, projectors, shifted):
    first_step = hamiltonian(bands_now, projectors, shifted).astype(jnp.bfloat16)
    return 2.0 * hamiltonian(first_step, projectors, shifted) - bands_now.astype(jnp.float32)


def body(orbitals, projectors, potential):
    local_rows = orbitals.shape[1]
    grid_count = local_rows * lax.axis_size("dom") * lax.axis_size("vec")
    shifted = potential - CENTER
    panel_list = [orbitals]
    seconds = [chebyshev(bands_now, projectors, shifted) for bands_now in panel_list]
    second = seconds[0]
    square_sum = lax.psum(jnp.sum(second * second, axis=1), ("dom", "vec"))
    normed_list = second * lax.rsqrt(square_sum / grid_count + EPSILON)[:, None]
    return normed_list.astype(jnp.bfloat16)


def solution(mesh):
    return jax.shard_map(
        body,
        mesh=mesh,
        in_specs=(P(None, ("dom", "vec")), P("dom", "vec"), P(("dom", "vec"))),
        out_specs=P(None, ("dom", "vec")),
        check_vma=False,
    )
```

profile of v0, /device:TPU:0, one launch (start us, length us, event | category | flops | bytes accessed | tf_op | source)
XLA Modules:
  0.0 294.5 jit_solution(7076762438744303975)
XLA Ops:
  6.5 0.0 copy-start
  6.5 0.0 all-gather.3.cloned.1.call-start
  6.5 0.7 all-gather.3.cloned.1.call-update
  7.3 0.0 reduce-scatter.3.cloned.1.call-start
  7.3 25.6 %all-gather.3.cloned.1.call-done = bf16[128,4096]{1,0:T(8,128)(2,1)} async-done(((bf16[128,2048]{1,0:T(8,128)(2,1)}), bf16[128,4096]{1,0:T(8,128)(2,1)}) %all-gather.3.cloned.1.call-update) | async-done | bytes 1048592 | tf_op jit(solution)/shard_map/all_gather | solution.py:13
  32.9 0.0 copy-done
  32.9 1.7 fusion.7
  34.6 61.8 %all-reduce.2 = bf16[128,256]{1,0:T(8,128)(2,1)S(1)} all-reduce(f32[128,256]{1,0:T(8,128)S(1)} %fusion.7), channel_id=1, replica_groups=mesh['dom'=16,'vec'=2] {'dom'}, use_global_device_ids=true, to_apply=%region_0.0 | all-reduce | flops 32768 | bytes 196608 | tf_op jit(solution)/shard_map/psum | solution.py:17
  96.4 2.2 fusion.10
  98.6 0.0 copy-start.3
  98.6 0.0 copy-start.1
  98.6 0.0 reduce-scatter.3.cloned.1.call-update
  98.6 0.0 all-gather.5.cloned.1.call-start
  98.7 0.6 copy-done.3
  99.3 27.8 %reduce-scatter.3.cloned.1.call-done = f32[128,2048]{1,0:T(8,128)} async-done(((f32[128,4096]{1,0:T(8,128)}), f32[128,2048]{1,0:T(8,128)}) %reduce-scatter.3.cloned.1.call-update) | async-done | bytes 1048592 | tf_op jit(solution)/shard_map/reduce_scatter | solution.py:21
  127.1 0.0 copy-done.1
  127.1 2.2 fusion.2
  129.2 0.0 all-gather.5.cloned.1.call-update
  129.3 0.0 reduce-scatter.5.cloned.1.call-start
  129.3 21.4 %all-gather.5.cloned.1.call-done = bf16[128,4096]{1,0:T(8,128)(2,1)} async-done(((bf16[128,2048]{1,0:T(8,128)(2,1)}), bf16[128,4096]{1,0:T(8,128)(2,1)}) %all-gather.5.cloned.1.call-update) | async-done | bytes 1048592 | tf_op jit(solution)/shard_map/all_gather | solution.py:13
  150.7 1.7 fusion.8
  152.4 61.8 %all-reduce.3 = bf16[128,256]{1,0:T(8,128)(2,1)S(1)} all-reduce(f32[128,256]{1,0:T(8,128)S(1)} %fusion.8), channel_id=1, replica_groups=mesh['dom'=16,'vec'=2] {'dom'}, use_global_device_ids=true, to_apply=%region_2.0 | all-reduce | flops 32768 | bytes 196608 | tf_op jit(solution)/shard_map/psum | solution.py:17
  214.2 2.2 fusion.9
  216.4 0.0 copy-start.2
  216.4 0.0 reduce-scatter.5.cloned.1.call-update
  216.4 28.4 %reduce-scatter.5.cloned.1.call-done = f32[128,2048]{1,0:T(8,128)} async-done(((f32[128,4096]{1,0:T(8,128)}), f32[128,2048]{1,0:T(8,128)}) %reduce-scatter.5.cloned.1.call-update) | async-done | bytes 1048592 | tf_op jit(solution)/shard_map/reduce_scatter | solution.py:21
  244.8 0.0 copy-done.2
  244.8 1.6 multiply_reduce_fusion
  246.4 39.3 %psum.23 = f32[128]{0:T(128)S(1)} all-reduce(f32[128]{0:T(128)S(1)} %multiply_reduce_fusion), channel_id=1, replica_groups=mesh['dom'=16,'vec'=2] {'dom','vec'}, use_global_device_ids=true, to_apply=%region_5.0 | all-reduce | flops 128 | bytes 1024 | tf_op jit(solution)/shard_map/psum | solution.py:37
  285.7 2.3 multiply_convert_fusion
  (2 shorter events, 0.0 us)
Async XLA Ops:
  6.5 26.4 %copy-start = (bf16[4096,256]{1,0:T(8,128)(2,1)S(1)}, bf16[4096,256]{1,0:T(8,128)(2,1)}, u32[]{:S(2)}) copy-start(bf16[4096,256]{1,0:T(8,128)(2,1)} %param.4) | copy-start | bytes 6291460
  6.5 26.4 %all-gather.3.cloned.1.call-start = ((), (), s32[]{:S(2)}) async-start(), calls=%async_computation.2 | async-start | bytes 1572864 | tf_op jit(solution)/shard_map/all_gather | solution.py:13
  7.3 119.8 %reduce-scatter.3.cloned.1.call-start = ((), (), s32[]{:S(2)}) async-start(), calls=%async_computation.3 | async-start | bytes 3145728 | tf_op jit(solution)/shard_map/reduce_scatter | solution.py:21
  98.6 0.7 copy-start.3
  98.6 28.5 %copy-start.1 = (bf16[128,2048]{1,0:T(8,128)(2,1)S(1)}, bf16[128,2048]{1,0:T(8,128)(2,1)}, u32[]{:S(2)}) copy-start(bf16[128,2048]{1,0:T(8,128)(2,1)} %param.3) | copy-start | bytes 1572868
  98.6 52.1 %all-gather.5.cloned.1.call-start = ((), (), s32[]{:S(2)}) async-start(), calls=%async_computation.4 | async-start | bytes 1572864 | tf_op jit(solution)/shard_map/all_gather | solution.py:13
  129.3 115.6 %reduce-scatter.5.cloned.1.call-start = ((), (), s32[]{:S(2)}) async-start(), calls=%async_computation.5 | async-start | bytes 3145728 | tf_op jit(solution)/shard_map/reduce_scatter | solution.py:21
  216.4 28.5 %copy-start.2 = (bf16[128,2048]{1,0:T(8,128)(2,1)S(1)}, bf16[128,2048]{1,0:T(8,128)(2,1)}, u32[]{:S(2)}) copy-start(bf16[128,2048]{1,0:T(8,128)(2,1)} %fusion.2) | copy-start | bytes 1572868
Sparse Core Ops, SparseCore 0:
  8.9 23.9 all-gather.2
  98.7 28.2 reduce-scatter.2
  129.4 21.2 all-gather.4
  216.5 28.2 reduce-scatter.4
where the time goes:
time: 295 us
  blocking collectives  163 us (55%)
  waiting for transfers between devices  104 us (35%)
  between operations  13.1 us (4%)
  matrix products  7.67 us (3%)
  other arithmetic  6.06 us (2%)
    psum x2, blocking collectives, hamiltonian(): intersection_b = lax.psum(partial_sum, 'dom').astype(jnp.bfloat16)  124 us
    reduce_scatter x2, waiting for transfers between devices, hamiltonian(): lax.psum_scatter(action_terms, 'vec', scatter_dimension=1, tiled=True)  56.2 us
    all_gather x2, waiting for transfers between devices, hamiltonian(): lax.all_gather(bands_now, 'vec', axis=1, tiled=True)  47 us
    psum x1, blocking collectives, body(): square_sum = lax.psum(jnp.sum(second * second, axis=1), ('dom', 'vec'))  39.3 us
  transfers between devices with their start and end apart: 4, of which 4 were waited for; matrix products, arithmetic and copies ran while one was open for 0% of the time, Pallas kernels for 0%

commit v1 on v0

v1 whole, which is shorter than its diff:
```python
import jax
import jax.numpy as jnp
from jax import lax
from jax.sharding import PartitionSpec as P

CENTER = 1.0
HALF_WIDTH = 1.5
EPSILON = 1e-06
F32 = jnp.float32
BF16 = jnp.bfloat16


def shift(value, axis, step):
    size = lax.axis_size(axis)
    return lax.ppermute(value, axis, [(i, (i + step) % size) for i in range(size)])


def sum_over(value, axis):
    size = lax.axis_size(axis)
    if size & (size - 1):
        return lax.psum(value, axis)
    bit = 1
    while bit < size:
        other = lax.ppermute(value.astype(BF16), axis, [(i, i ^ bit) for i in range(size)])
        value = value + other.astype(F32)
        bit *= 2
    return value


def dot(a, b):
    return jnp.dot(a, b, preferred_element_type=F32)


def dot_t(a, b):
    return lax.dot_general(a, b, (((1,), (1,)), ((), ())), preferred_element_type=F32)


def body(orbitals, projectors, potential):
    groups = lax.axis_size("vec")
    mine = lax.axis_index("vec")
    points = orbitals.shape[1]
    axes = ("dom", "vec")
    devices = lax.axis_size(axes)
    shifted = (potential - CENTER)[None, :]

    def rows_of(group):
        return lax.dynamic_slice_in_dim(projectors, group * points, points, 0)

    far_bands = [shift(orbitals, "vec", s) for s in range(1, groups)]
    own = rows_of(mine)
    far_rows = [rows_of((mine + s) % groups) for s in range(1, groups)]
    blocks = [own] + [shift(far_rows[s - 1], "vec", s) for s in range(1, groups)]

    partial = dot(orbitals, own)
    for s in range(1, groups):
        partial = partial + dot(far_bands[s - 1], far_rows[groups - s - 1])
    first_b = sum_over(partial, "dom").astype(BF16)
    firsts = [first_b] + [shift(first_b, "vec", s) for s in range(1, groups)]

    bands = orbitals.astype(F32)
    actions = sum(dot_t(c, b) for c, b in zip(firsts, blocks))
    step = ((shifted * bands - actions) / HALF_WIDTH).astype(BF16)

    partial = dot(step, own)
    for s in range(1, groups):
        partial = partial + shift(dot(step, blocks[s]).astype(BF16), "vec", groups - s).astype(F32)
    second_b = sum_over(partial, "dom").astype(BF16)
    seconds = [second_b] + [shift(second_b, "vec", s) for s in range(1, groups)]

    actions = sum(dot_t(c, b) for c, b in zip(seconds, blocks))
    second = 2.0 * ((shifted * step.astype(F32) - actions) / HALF_WIDTH) - bands
    square = jnp.sum(second * second, axis=1)
    square = lax.all_to_all(jnp.broadcast_to(square, (devices, 1) + square.shape), axes, 0, 0)
    square_sum = jnp.sum(square, axis=(0, 1))
    scale = lax.rsqrt(square_sum / (points * devices) + EPSILON)
    return (second * scale[:, None]).astype(BF16)


def solution(mesh):
    return jax.shard_map(
        body,
        mesh=mesh,
        in_specs=(P(None, ("dom", "vec")), P("dom", "vec"), P(("dom", "vec"))),
        out_specs=P(None, ("dom", "vec")),
        check_vma=False,
    )
```

time: 295 us -> 85.5 us (0.29)
  blocking collectives: 163 us -> 12.5 us
  waiting for transfers between devices: 104 us -> 45.8 us
  starting transfers between devices: 0.13 us -> 20.9 us
  between operations: 13.1 us -> 0.15 us
  other arithmetic: 6.06 us -> 1.17 us
    psum x3 -> x0, blocking collectives: 163 us -> none  [the longest x2 124 us: hamiltonian(): intersection_b = lax.psum(partial_sum, 'dom').astype(jnp.bfloat16)]
    reduce_scatter x2 -> x0, waiting for transfers between devices: 56.2 us -> none  [hamiltonian(): lax.psum_scatter(action_terms, 'vec', scatter_dimension=1, tiled=True)]
    all_gather x2 -> x0, waiting for transfers between devices: 47 us -> none  [hamiltonian(): lax.all_gather(bands_now, 'vec', axis=1, tiled=True)]
    ppermute x0 -> x13, waiting for transfers between devices: none -> 45.8 us  [the longest x5 28.3 us: shift(): lax.ppermute(value, axis, [(i, (i + step) % size) for i in range(size)])]
    ppermute x0 -> x13, starting transfers between devices: none -> 20.9 us  [the longest x8 11.4 us: sum_over(): lax.ppermute(value.astype(BF16), axis, [(i, i ^ bit) for i in range(size)])]
    all_to_all x0 -> x1, blocking collectives: none -> 12.5 us  [body(): lax.all_to_all(jnp.broadcast_to(square, (devices, 1) + square.shape), axe...]
    convert_element_type x2 -> x9, other arithmetic: 4.47 us -> 1.14 us  [the longest x1 0.92 us: body(): return (second * scale[:, None]).astype(BF16)]
    dot_general x4 -> x8, matrix products: 7.67 us -> 4.74 us  [the longest x4 2.64 us: dot(): return jnp.dot(a, b, preferred_element_type=F32)]
  transfers between devices with their start and end apart: 4 -> 13, of which waited for: 4 -> 12; matrix products, arithmetic and copies ran while one was open for 0% -> 2% of each run, Pallas kernels for 0% -> 0%
where the time goes in v1:
time: 85.5 us; the launch traced here: 85.4 us
  waiting for transfers between devices  45.8 us (54%)
  starting transfers between devices  20.9 us (24%)
  blocking collectives  12.5 us (15%)
  matrix products  4.74 us (6%)
  other arithmetic  1.17 us (1%)
    ppermute x5, waiting for transfers between devices, shift(): lax.ppermute(value, axis, [(i, (i + step) % size) for i in range(size)])  28.3 us
    ppermute x8, waiting for transfers between devices, sum_over(): lax.ppermute(value.astype(BF16), axis, [(i, i ^ bit) for i in range(size)])  17.5 us
    all_to_all x1, blocking collectives, body(): lax.all_to_all(jnp.broadcast_to(square, (devices, 1) + square.shape), axe...  12.5 us
    ppermute x8, starting transfers between devices, sum_over(): lax.ppermute(value.astype(BF16), axis, [(i, i ^ bit) for i in range(size)])  11.4 us
    ppermute x5, starting transfers between devices, shift(): lax.ppermute(value, axis, [(i, (i + step) % size) for i in range(size)])  9.49 us
    dot_general x4, matrix products, dot(): return jnp.dot(a, b, preferred_element_type=F32)  2.64 us
    dot_general x4, matrix products, dot_t(): lax.dot_general(a, b, (((1,), (1,)), ((), ())), preferred_element_type=F32)  2.1 us
  transfers between devices with their start and end apart: 13, of which 12 were waited for; matrix products, arithmetic and copies ran while one was open for 2% of the time, Pallas kernels for 0%

profile of v1, /device:TPU:0, one launch (start us, length us, event | category | flops | bytes accessed | tf_op | source)
XLA Modules:
  0.0 85.4 jit_solution(2366266545680398751)
XLA Ops:
  0.0 0.0 copy-start
  0.0 3.0 %collective-permute-start = (bf16[128,2048]{1,0:T(8,128)(2,1)}, bf16[128,2048]{1,0:T(8,128)(2,1)S(1)}, u32[]{:S(2)}, u32[]{:S(2)}) collective-permute-start(bf16[128,2048]{1,0:T(8,128)(2,1)} %param.3), channel_id=1, source_target_pairs={{0,1},{1,0},{2,3},{3,2},{4,5},{5,4},{6,7},{7,6},{8,9},{9,8},{10,11... | collective-permute-start | bytes 1572872 | tf_op jit(solution)/shard_map/ppermute | solution.py:15
  3.0 0.0 copy-done
  3.0 1.5 %fusion.11 = f32[256,128]{1,0:T(8,128)S(1)} fusion(bf16[128,2048]{1,0:T(8,128)(2,1)} %param.3, bf16[4096,256]{1,0:T(8,128)(2,1)S(1)} %copy-done, s32[]{:T(128)S(6)} %select_n.13), kind=kOutput, calls=%fused_computation.18 | convolution fusion | flops 134217728 | bytes 1703940 | tf_op jit(solution)/shard_map/dot_general | solution.py:31
  4.5 0.1 constant_dynamic-slice_fusion
  4.6 0.0 copy-start.2
  4.6 10.5 %collective-permute-done = bf16[128,2048]{1,0:T(8,128)(2,1)S(1)} collective-permute-done((bf16[128,2048]{1,0:T(8,128)(2,1)}, bf16[128,2048]{1,0:T(8,128)(2,1)S(1)}, u32[]{:S(2)}, u32[]{:S(2)}) %collective-permute-start) | collective-permute-done | bytes 524320 | tf_op jit(solution)/shard_map/ppermute | solution.py:15
  15.1 0.5 fusion.24
  15.6 0.0 copy-start.1
  15.6 0.1 collective-permute-start.1
  15.7 1.2 %collective-permute-done.1 = bf16[128,256]{0,1:T(8,128)(2,1)S(1)} collective-permute-done((bf16[128,256]{0,1:T(8,128)(2,1)S(1)}, bf16[128,256]{0,1:T(8,128)(2,1)S(1)}, u32[]{:S(2)}, u32[]{:S(2)}) %collective-permute-start.1) | collective-permute-done | bytes 65568 | tf_op jit(solution)/shard_map/ppermute | solution.py:24
  17.0 1.8 %collective-permute-start.2 = (bf16[128,256]{0,1:T(8,128)(2,1)S(1)}, bf16[128,256]{0,1:T(8,128)(2,1)S(1)}, u32[]{:S(2)}, u32[]{:S(2)}) collective-permute-start(bf16[128,256]{0,1:T(8,128)(2,1)S(1)} %fusion.13), channel_id=1, source_target_pairs={{0,4},{2,6},{4,0},{6,2},{8,12},{10,14},{12,8},{14,10},{16,20},{18,... | collective-permute-start | bytes 196616 | tf_op jit(solution)/shard_map/ppermute | solution.py:24
  18.7 1.5 %collective-permute-start.6 = (bf16[2048,256]{1,0:T(8,128)(2,1)S(1)}, bf16[2048,256]{1,0:T(8,128)(2,1)S(1)}, u32[]{:S(2)}, u32[]{:S(2)}) collective-permute-start(bf16[2048,256]{1,0:T(8,128)(2,1)S(1)} %constant_dynamic-slice_fusion), channel_id=1, source_target_pairs={{0,1},{1,0},{2,3},{3,2},{4,5},{5,4},{6,7},{7,6},{8,9},{9,8},{10,11... | collective-permute-start | bytes 3145736 | tf_op jit(solution)/shard_map/ppermute | solution.py:15
  20.3 1.0 %collective-permute-done.2 = bf16[128,256]{0,1:T(8,128)(2,1)S(1)} collective-permute-done((bf16[128,256]{0,1:T(8,128)(2,1)S(1)}, bf16[128,256]{0,1:T(8,128)(2,1)S(1)}, u32[]{:S(2)}, u32[]{:S(2)}) %collective-permute-start.2) | collective-permute-done | bytes 65568 | tf_op jit(solution)/shard_map/ppermute | solution.py:24
  21.3 1.9 %collective-permute-start.3 = (bf16[128,256]{0,1:T(8,128)(2,1)S(1)}, bf16[128,256]{0,1:T(8,128)(2,1)S(1)}, u32[]{:S(2)}, u32[]{:S(2)}) collective-permute-start(bf16[128,256]{0,1:T(8,128)(2,1)S(1)} %fusion.22), channel_id=1, source_target_pairs={{0,8},{2,10},{4,12},{6,14},{8,0},{10,2},{12,4},{14,6},{16,24},{18,... | collective-permute-start | bytes 196616 | tf_op jit(solution)/shard_map/ppermute | solution.py:24
  23.2 2.5 %collective-permute-done.3 = bf16[128,256]{0,1:T(8,128)(2,1)S(1)} collective-permute-done((bf16[128,256]{0,1:T(8,128)(2,1)S(1)}, bf16[128,256]{0,1:T(8,128)(2,1)S(1)}, u32[]{:S(2)}, u32[]{:S(2)}) %collective-permute-start.3) | collective-permute-done | bytes 65568 | tf_op jit(solution)/shard_map/ppermute | solution.py:24
  25.7 2.9 %collective-permute-start.4 = (bf16[128,256]{0,1:T(8,128)(2,1)S(1)}, bf16[128,256]{0,1:T(8,128)(2,1)S(1)}, u32[]{:S(2)}, u32[]{:S(2)}) collective-permute-start(bf16[128,256]{0,1:T(8,128)(2,1)S(1)} %fusion.14), channel_id=1, source_target_pairs={{0,16},{2,18},{4,20},{6,22},{8,24},{10,26},{12,28},{14,30},{16,0},... | collective-permute-start | bytes 196616 | tf_op jit(solution)/shard_map/ppermute | solution.py:24
  28.6 2.3 %collective-permute-done.4 = bf16[128,256]{0,1:T(8,128)(2,1)S(1)} collective-permute-done((bf16[128,256]{0,1:T(8,128)(2,1)S(1)}, bf16[128,256]{0,1:T(8,128)(2,1)S(1)}, u32[]{:S(2)}, u32[]{:S(2)}) %collective-permute-start.4) | collective-permute-done | bytes 65568 | tf_op jit(solution)/shard_map/ppermute | solution.py:24
  31.0 1.8 %collective-permute-start.5 = (bf16[128,256]{0,1:T(8,128)(2,1)S(1)}, bf16[128,256]{0,1:T(8,128)(2,1)S(1)}, u32[]{:S(2)}, u32[]{:S(2)}) collective-permute-start(bf16[128,256]{0,1:T(8,128)(2,1)S(1)} %add_convert_fusion.1), channel_id=1, source_target_pairs={{0,1},{1,0},{2,3},{3,2},{4,5},{5,4},{6,7},{7,6},{8,9},{9,8},{10,11... | collective-permute-start | bytes 196616 | tf_op jit(solution)/shard_map/ppermute | solution.py:15
  32.8 0.0 copy-done.2
  32.8 12.3 %collective-permute-done.5 = bf16[128,256]{0,1:T(8,128)(2,1)S(1)} collective-permute-done((bf16[128,256]{0,1:T(8,128)(2,1)S(1)}, bf16[128,256]{0,1:T(8,128)(2,1)S(1)}, u32[]{:S(2)}, u32[]{:S(2)}) %collective-permute-start.5) | collective-permute-done | bytes 65568 | tf_op jit(solution)/shard_map/ppermute | solution.py:15
  45.1 0.0 collective-permute-done.6
  45.1 0.5 fusion.25
  45.6 0.0 copy-done.1
  45.6 0.5 fusion.5
  46.1 0.3 convolution_convert_fusion
  46.4 1.6 %collective-permute-start.7 = (bf16[128,256]{1,0:T(8,128)(2,1)S(1)}, bf16[128,256]{1,0:T(8,128)(2,1)S(1)}, u32[]{:S(2)}, u32[]{:S(2)}) collective-permute-start(bf16[128,256]{1,0:T(8,128)(2,1)S(1)} %convolution_convert_fusion), channel_id=1, source_target_pairs={{0,1},{1,0},{2,3},{3,2},{4,5},{5,4},{6,7},{7,6},{8,9},{9,8},{10,11... | collective-permute-start | bytes 196616 | tf_op jit(solution)/shard_map/ppermute | solution.py:15
  48.0 2.7 %collective-permute-done.7 = bf16[128,256]{1,0:T(8,128)(2,1)S(1)} collective-permute-done((bf16[128,256]{1,0:T(8,128)(2,1)S(1)}, bf16[128,256]{1,0:T(8,128)(2,1)S(1)}, u32[]{:S(2)}, u32[]{:S(2)}) %collective-permute-start.7) | collective-permute-done | bytes 65568 | tf_op jit(solution)/shard_map/ppermute | solution.py:15
  50.7 0.3 fusion.15
  51.1 0.1 collective-permute-start.8
  51.1 1.2 %collective-permute-done.8 = bf16[128,256]{1,0:T(8,128)(2,1)S(1)} collective-permute-done((bf16[128,256]{1,0:T(8,128)(2,1)S(1)}, bf16[128,256]{1,0:T(8,128)(2,1)S(1)}, u32[]{:S(2)}, u32[]{:S(2)}) %collective-permute-start.8) | collective-permute-done | bytes 65568 | tf_op jit(solution)/shard_map/ppermute | solution.py:24
  52.4 0.4 collective-permute-start.9
  52.8 3.9 %collective-permute-done.9 = bf16[128,256]{1,0:T(8,128)(2,1)S(1)} collective-permute-done((bf16[128,256]{1,0:T(8,128)(2,1)S(1)}, bf16[128,256]{1,0:T(8,128)(2,1)S(1)}, u32[]{:S(2)}, u32[]{:S(2)}) %collective-permute-start.9) | collective-permute-done | bytes 65568 | tf_op jit(solution)/shard_map/ppermute | solution.py:24
  56.8 1.6 %collective-permute-start.10 = (bf16[128,256]{1,0:T(8,128)(2,1)S(1)}, bf16[128,256]{1,0:T(8,128)(2,1)S(1)}, u32[]{:S(2)}, u32[]{:S(2)}) collective-permute-start(bf16[128,256]{1,0:T(8,128)(2,1)S(1)} %fusion.16), channel_id=1, source_target_pairs={{0,8},{2,10},{4,12},{6,14},{8,0},{10,2},{12,4},{14,6},{16,24},{18,... | collective-permute-start | bytes 196616 | tf_op jit(solution)/shard_map/ppermute | solution.py:24
  58.4 2.7 %collective-permute-done.10 = bf16[128,256]{1,0:T(8,128)(2,1)S(1)} collective-permute-done((bf16[128,256]{1,0:T(8,128)(2,1)S(1)}, bf16[128,256]{1,0:T(8,128)(2,1)S(1)}, u32[]{:S(2)}, u32[]{:S(2)}) %collective-permute-start.10) | collective-permute-done | bytes 65568 | tf_op jit(solution)/shard_map/ppermute | solution.py:24
  61.1 2.7 %collective-permute-start.11 = (bf16[128,256]{1,0:T(8,128)(2,1)S(1)}, bf16[128,256]{1,0:T(8,128)(2,1)S(1)}, u32[]{:S(2)}, u32[]{:S(2)}) collective-permute-start(bf16[128,256]{1,0:T(8,128)(2,1)S(1)} %fusion.17), channel_id=1, source_target_pairs={{0,16},{2,18},{4,20},{6,22},{8,24},{10,26},{12,28},{14,30},{16,0},... | collective-permute-start | bytes 196616 | tf_op jit(solution)/shard_map/ppermute | solution.py:24
  63.8 2.6 %collective-permute-done.11 = bf16[128,256]{1,0:T(8,128)(2,1)S(1)} collective-permute-done((bf16[128,256]{1,0:T(8,128)(2,1)S(1)}, bf16[128,256]{1,0:T(8,128)(2,1)S(1)}, u32[]{:S(2)}, u32[]{:S(2)}) %collective-permute-start.11) | collective-permute-done | bytes 65568 | tf_op jit(solution)/shard_map/ppermute | solution.py:24
  66.4 1.6 %collective-permute-start.12 = (bf16[128,256]{1,0:T(8,128)(2,1)S(1)}, bf16[128,256]{1,0:T(8,128)(2,1)S(1)}, u32[]{:S(2)}, u32[]{:S(2)}) collective-permute-start(bf16[128,256]{1,0:T(8,128)(2,1)S(1)} %add_convert_fusion), channel_id=1, source_target_pairs={{0,1},{1,0},{2,3},{3,2},{4,5},{5,4},{6,7},{7,6},{8,9},{9,8},{10,11... | collective-permute-start | bytes 196616 | tf_op jit(solution)/shard_map/ppermute | solution.py:15
  68.0 2.7 %collective-permute-done.12 = bf16[128,256]{1,0:T(8,128)(2,1)S(1)} collective-permute-done((bf16[128,256]{1,0:T(8,128)(2,1)S(1)}, bf16[128,256]{1,0:T(8,128)(2,1)S(1)}, u32[]{:S(2)}, u32[]{:S(2)}) %collective-permute-start.12) | collective-permute-done | bytes 65568 | tf_op jit(solution)/shard_map/ppermute | solution.py:15
  70.7 0.5 fusion.26
  71.2 0.6 multiply_reduce_fusion
  71.9 12.5 %all_to_all.5 = f32[32,1,128]{2,1,0:T(1,128)S(1)} all-to-all(f32[32,1,128]{2,1,0:T(1,128)S(1)} %broadcast_in_dim.2), channel_id=1, replica_groups=mesh['dom'=16,'vec'=2] {'dom','vec'}, dimensions={0} | all-to-all | bytes 32768 | tf_op jit(solution)/shard_map/all_to_all | solution.py:73
  84.4 0.9 %multiply_convert_fusion = bf16[128,2048]{1,0:T(8,128)(2,1)} fusion(f32[128,2048]{1,0:T(8,128)S(1)} %get-tuple-element.12, f32[128]{0:T(128)S(1)} %add_rsqrt_fusion), kind=kLoop, calls=%fused_computation.12 | loop fusion | flops 524288 | bytes 1573376 | tf_op jit(solution)/shard_map/convert_element_type | solution.py:76
  (12 shorter events, 0.3 us)
Async XLA Ops:
  0.0 3.0 %copy-start = (bf16[4096,256]{1,0:T(8,128)(2,1)S(1)}, bf16[4096,256]{1,0:T(8,128)(2,1)}, u32[]{:S(2)}) copy-start(bf16[4096,256]{1,0:T(8,128)(2,1)} %param.4) | copy-start | bytes 6291460
  0.0 15.1 %collective-permute-start = (bf16[128,2048]{1,0:T(8,128)(2,1)}, bf16[128,2048]{1,0:T(8,128)(2,1)S(1)}, u32[]{:S(2)}, u32[]{:S(2)}) collective-permute-start(bf16[128,2048]{1,0:T(8,128)(2,1)} %param.3), channel_id=1, source_target_pairs={{0,1},{1,0},{2,3},{3,2},{4,5},{5,4},{6,7},{7,6},{8,9},{9,8},{10,11... | collective-permute-start | bytes 1572872 | tf_op jit(solution)/shard_map/ppermute | solution.py:15
  4.6 28.1 %copy-start.2 = (f32[2048]{0:T(1024)S(1)}, f32[2048]{0:T(1024)}, u32[]{:S(2)}) copy-start(f32[2048]{0:T(1024)} %param.5) | copy-start | bytes 24580
  15.6 30.0 %copy-start.1 = (bf16[128,2048]{1,0:T(8,128)(2,1)S(1)}, bf16[128,2048]{1,0:T(8,128)(2,1)}, u32[]{:S(2)}) copy-start(bf16[128,2048]{1,0:T(8,128)(2,1)} %param.3) | copy-start | bytes 1572868
  15.6 1.3 %collective-permute-start.1 = (bf16[128,256]{0,1:T(8,128)(2,1)S(1)}, bf16[128,256]{0,1:T(8,128)(2,1)S(1)}, u32[]{:S(2)}, u32[]{:S(2)}) collective-permute-start(bf16[128,256]{0,1:T(8,128)(2,1)S(1)} %get-tuple-element.7), channel_id=1, source_target_pairs={{0,2},{2,0},{4,6},{6,4},{8,10},{10,8},{12,14},{14,12},{16,18},{18,... | collective-permute-start | bytes 196616 | tf_op jit(solution)/shard_map/ppermute | solution.py:24
  17.0 4.3 %collective-permute-start.2 = (bf16[128,256]{0,1:T(8,128)(2,1)S(1)}, bf16[128,256]{0,1:T(8,128)(2,1)S(1)}, u32[]{:S(2)}, u32[]{:S(2)}) collective-permute-start(bf16[128,256]{0,1:T(8,128)(2,1)S(1)} %fusion.13), channel_id=1, source_target_pairs={{0,4},{2,6},{4,0},{6,2},{8,12},{10,14},{12,8},{14,10},{16,20},{18,... | collective-permute-start | bytes 196616 | tf_op jit(solution)/shard_map/ppermute | solution.py:24
  18.7 26.3 %collective-permute-start.6 = (bf16[2048,256]{1,0:T(8,128)(2,1)S(1)}, bf16[2048,256]{1,0:T(8,128)(2,1)S(1)}, u32[]{:S(2)}, u32[]{:S(2)}) collective-permute-start(bf16[2048,256]{1,0:T(8,128)(2,1)S(1)} %constant_dynamic-slice_fusion), channel_id=1, source_target_pairs={{0,1},{1,0},{2,3},{3,2},{4,5},{5,4},{6,7},{7,6},{8,9},{9,8},{10,11... | collective-permute-start | bytes 3145736 | tf_op jit(solution)/shard_map/ppermute | solution.py:15
  21.3 4.3 %collective-permute-start.3 = (bf16[128,256]{0,1:T(8,128)(2,1)S(1)}, bf16[128,256]{0,1:T(8,128)(2,1)S(1)}, u32[]{:S(2)}, u32[]{:S(2)}) collective-permute-start(bf16[128,256]{0,1:T(8,128)(2,1)S(1)} %fusion.22), channel_id=1, source_target_pairs={{0,8},{2,10},{4,12},{6,14},{8,0},{10,2},{12,4},{14,6},{16,24},{18,... | collective-permute-start | bytes 196616 | tf_op jit(solution)/shard_map/ppermute | solution.py:24
  25.7 5.2 %collective-permute-start.4 = (bf16[128,256]{0,1:T(8,128)(2,1)S(1)}, bf16[128,256]{0,1:T(8,128)(2,1)S(1)}, u32[]{:S(2)}, u32[]{:S(2)}) collective-permute-start(bf16[128,256]{0,1:T(8,128)(2,1)S(1)} %fusion.14), channel_id=1, source_target_pairs={{0,16},{2,18},{4,20},{6,22},{8,24},{10,26},{12,28},{14,30},{16,0},... | collective-permute-start | bytes 196616 | tf_op jit(solution)/shard_map/ppermute | solution.py:24
  31.0 14.1 %collective-permute-start.5 = (bf16[128,256]{0,1:T(8,128)(2,1)S(1)}, bf16[128,256]{0,1:T(8,128)(2,1)S(1)}, u32[]{:S(2)}, u32[]{:S(2)}) collective-permute-start(bf16[128,256]{0,1:T(8,128)(2,1)S(1)} %add_convert_fusion.1), channel_id=1, source_target_pairs={{0,1},{1,0},{2,3},{3,2},{4,5},{5,4},{6,7},{7,6},{8,9},{9,8},{10,11... | collective-permute-start | bytes 196616 | tf_op jit(solution)/shard_map/ppermute | solution.py:15
  46.4 4.3 %collective-permute-start.7 = (bf16[128,256]{1,0:T(8,128)(2,1)S(1)}, bf16[128,256]{1,0:T(8,128)(2,1)S(1)}, u32[]{:S(2)}, u32[]{:S(2)}) collective-permute-start(bf16[128,256]{1,0:T(8,128)(2,1)S(1)} %convolution_convert_fusion), channel_id=1, source_target_pairs={{0,1},{1,0},{2,3},{3,2},{4,5},{5,4},{6,7},{7,6},{8,9},{9,8},{10,11... | collective-permute-start | bytes 196616 | tf_op jit(solution)/shard_map/ppermute | solution.py:15
  51.1 1.3 %collective-permute-start.8 = (bf16[128,256]{1,0:T(8,128)(2,1)S(1)}, bf16[128,256]{1,0:T(8,128)(2,1)S(1)}, u32[]{:S(2)}, u32[]{:S(2)}) collective-permute-start(bf16[128,256]{1,0:T(8,128)(2,1)S(1)} %get-tuple-element.9), channel_id=1, source_target_pairs={{0,2},{2,0},{4,6},{6,4},{8,10},{10,8},{12,14},{14,12},{16,18},{18,... | collective-permute-start | bytes 196616 | tf_op jit(solution)/shard_map/ppermute | solution.py:24
  52.4 4.3 %collective-permute-start.9 = (bf16[128,256]{1,0:T(8,128)(2,1)S(1)}, bf16[128,256]{1,0:T(8,128)(2,1)S(1)}, u32[]{:S(2)}, u32[]{:S(2)}) collective-permute-start(bf16[128,256]{1,0:T(8,128)(2,1)S(1)} %get-tuple-element.5), channel_id=1, source_target_pairs={{0,4},{2,6},{4,0},{6,2},{8,12},{10,14},{12,8},{14,10},{16,20},{18,... | collective-permute-start | bytes 196616 | tf_op jit(solution)/shard_map/ppermute | solution.py:24
  56.8 4.3 %collective-permute-start.10 = (bf16[128,256]{1,0:T(8,128)(2,1)S(1)}, bf16[128,256]{1,0:T(8,128)(2,1)S(1)}, u32[]{:S(2)}, u32[]{:S(2)}) collective-permute-start(bf16[128,256]{1,0:T(8,128)(2,1)S(1)} %fusion.16), channel_id=1, source_target_pairs={{0,8},{2,10},{4,12},{6,14},{8,0},{10,2},{12,4},{14,6},{16,24},{18,... | collective-permute-start | bytes 196616 | tf_op jit(solution)/shard_map/ppermute | solution.py:24
  61.1 5.2 %collective-permute-start.11 = (bf16[128,256]{1,0:T(8,128)(2,1)S(1)}, bf16[128,256]{1,0:T(8,128)(2,1)S(1)}, u32[]{:S(2)}, u32[]{:S(2)}) collective-permute-start(bf16[128,256]{1,0:T(8,128)(2,1)S(1)} %fusion.17), channel_id=1, source_target_pairs={{0,16},{2,18},{4,20},{6,22},{8,24},{10,26},{12,28},{14,30},{16,0},... | collective-permute-start | bytes 196616 | tf_op jit(solution)/shard_map/ppermute | solution.py:24
  66.4 4.3 %collective-permute-start.12 = (bf16[128,256]{1,0:T(8,128)(2,1)S(1)}, bf16[128,256]{1,0:T(8,128)(2,1)S(1)}, u32[]{:S(2)}, u32[]{:S(2)}) collective-permute-start(bf16[128,256]{1,0:T(8,128)(2,1)S(1)} %add_convert_fusion), channel_id=1, source_target_pairs={{0,1},{1,0},{2,3},{3,2},{4,5},{5,4},{6,7},{7,6},{8,9},{9,8},{10,11... | collective-permute-start | bytes 196616 | tf_op jit(solution)/shard_map/ppermute | solution.py:15
